TPU v7x, 32 devices: a whole 2x2x4 slice. The times are simulated.
32 devices in a mesh: dp: 8 (over z, y), tp: 4 (over x, core).
Axes of the slice: x: 2, y: 2, z: 4, core: 2. Of those that a mesh axis runs over, the one named last changes fastest.
Arguments:
- q_latent: bfloat16 [1024, 4, 1536], P('dp'), may hold values from -6 to 6
- new_latent: bfloat16 [1024, 4, 512], P('dp'), may hold values from -6 to 6
- new_rope: bfloat16 [1024, 4, 64], P('dp'), may hold values from -6 to 6
- cache_latent: bfloat16 [1024, 256, 512], P('dp'), may hold values from -6 to 6
- cache_rope: bfloat16 [1024, 64, 256], P('dp'), may hold values from -1200 to 1200
- lengths: int32 [1024], P('dp'), may hold values from 1 to 256
- assignment: int32 [8, 128], P('dp'), may hold values from 0 to 127, each once within a row
- w_uq: float32 [1536, 12288], P(('dp', 'tp')), may hold values from -0.15625 to 0.15625
- w_uk: float32 [512, 8192], P(('dp', 'tp')), may hold values from -0.75 to 0.75
- w_uv: float32 [512, 8192], P(('dp', 'tp')), may hold values from -0.25 to 0.25
- w_o: float32 [8192, 7168], P(None, ('dp', 'tp')), may hold values from -0.0625 to 0.0625
Outputs:
- attention_out: bfloat16 [1024, 4, 7168], P('dp', None, 'tp')
- weight_norm: float32 [1], replicated
Inputs may be any that keep to these rules, and one draw needn't show every extreme that they name: Each row of assignment is a permutation of 0 to 127.
All inputs are finite; a program needn't handle non-finite values.
Results may differ from a plain program's by a relative error of at most 0.006.
The roundings to bfloat16 on the way count: a program that leaves them out, or rounds other values in their place, can miss the bound.
Values may be sent and summed in bfloat16 or wider, within the bound.
A program may use at most 256 MiB of HBM per device.

v0:
```python
import jax
import jax.numpy as jnp
from jax import lax
from jax.sharding import PartitionSpec as P

D = 7168
QRANK = 1536
KVRANK = 512
NOPE = 128
ROPE = 64
VDIM = 128
HEADS = 64
NEWTOK = 4
CACHE = 256


def widen(values):
    return lax.optimization_barrier(values).astype(jnp.float32)


def rotate_half(values, positions):
    half_width = values.shape[-1] // 2
    frequency = 10000.0 ** (-jnp.arange(half_width, dtype=jnp.float32) / half_width)
    angles = positions.astype(jnp.float32)[:, :, None, None] * frequency
    cosine = jnp.cos(angles)
    sine_part = jnp.sin(angles)
    lower_half = values[..., :half_width]
    upper_half = values[..., half_width:]
    return jnp.concatenate(
        [
            lower_half * cosine - upper_half * sine_part,
            upper_half * cosine + lower_half * sine_part,
        ],
        axis=-1,
    )


def shards(
    q_latent,
    new_latent,
    new_rope,
    cache_latent,
    cache_rope,
    lengths,
    assignment,
    w_uq,
    w_uk,
    w_uv,
    w_o,
):
    local_squares = (
        jnp.sum(w_uq * w_uq) + jnp.sum(w_uk * w_uk) + jnp.sum(w_uv * w_uv) + jnp.sum(w_o * w_o)
    )
    squares_total = lax.psum(local_squares, ("dp", "tp"))
    weight_norm = jnp.sqrt(squares_total / (HEADS * (NOPE + ROPE) + 2 * HEADS * NOPE + D)).reshape(
        1
    )
    query_cast = w_uq.astype(jnp.bfloat16)
    key_cast = w_uk.astype(jnp.bfloat16)
    value_cast = w_uv.astype(jnp.bfloat16)
    gathered = (
        lax.all_gather(query_cast[None], "dp", axis=0, tiled=True),
        lax.all_gather(key_cast[None], "dp", axis=0, tiled=True),
        lax.all_gather(value_cast[None], "dp", axis=0, tiled=True),
    )
    mixed = (
        lax.all_to_all(gathered[0], "tp", split_axis=2, concat_axis=1, tiled=True),
        lax.all_to_all(gathered[1], "tp", split_axis=2, concat_axis=1, tiled=True),
        lax.all_to_all(gathered[2], "tp", split_axis=2, concat_axis=1, tiled=True),
    )
    query_up = mixed[0].reshape(-1, mixed[0].shape[2])
    key_up = mixed[1].reshape(-1, mixed[1].shape[2])
    value_up = mixed[2].reshape(-1, mixed[2].shape[2])
    out_cast = w_o.astype(jnp.bfloat16)
    seq_count = q_latent.shape[0]
    heads_here = key_up.shape[1] // NOPE
    selector = (assignment[0][:, None] == jnp.arange(seq_count, dtype=jnp.int32)[None, :]).astype(
        jnp.bfloat16
    )

    def to_slots(array):
        moved = jnp.dot(
            selector.T, array.reshape(seq_count, -1), preferred_element_type=jnp.float32
        )
        return moved.astype(jnp.bfloat16).reshape(array.shape)

    query_slots = to_slots(q_latent)
    latent_slots = to_slots(new_latent)
    rope_slots = to_slots(new_rope)
    projected = jnp.dot(
        query_slots.reshape(seq_count * NEWTOK, QRANK), query_up, preferred_element_type=jnp.float32
    )
    projected = projected.astype(jnp.bfloat16).reshape(seq_count, NEWTOK, heads_here, NOPE + ROPE)
    query_nope = projected[..., :NOPE]
    positions = lengths[:, None] + jnp.arange(NEWTOK, dtype=jnp.int32)[None, :]
    query_rot = rotate_half(widen(projected[..., NOPE:]), positions).astype(jnp.bfloat16)
    absorbed = jnp.einsum(
        "sqhn,chn->sqhc",
        query_nope,
        key_up.reshape(KVRANK, heads_here, NOPE),
        preferred_element_type=jnp.float32,
    ).astype(jnp.bfloat16)
    scale = (NOPE + ROPE) ** (-0.5)
    cache_scores = jnp.einsum(
        "sqhc,stc->sqht", absorbed, cache_latent, preferred_element_type=jnp.float32
    )
    cache_scores = (
        cache_scores
        + jnp.einsum("sqhr,srt->sqht", query_rot, cache_rope, preferred_element_type=jnp.float32)
    ) * scale
    valid = jnp.arange(CACHE, dtype=jnp.int32)[None, :] < lengths[:, None]
    cache_scores = jnp.where(valid[:, None, None, :], cache_scores, -jnp.inf)
    new_scores = jnp.einsum(
        "sqhc,skc->sqhk", absorbed, latent_slots, preferred_element_type=jnp.float32
    )
    new_scores = (
        new_scores
        + jnp.einsum("sqhr,skr->sqhk", query_rot, rope_slots, preferred_element_type=jnp.float32)
    ) * scale
    causal = jnp.arange(NEWTOK)[:, None] >= jnp.arange(NEWTOK)[None, :]
    new_scores = jnp.where(causal[None, :, None, :], new_scores, -jnp.inf)
    scores = jnp.concatenate([cache_scores, new_scores], axis=-1)
    largest = jnp.max(scores, axis=-1, keepdims=True)
    expo = jnp.exp(scores - largest)
    weights = (expo / jnp.sum(expo, axis=-1, keepdims=True)).astype(jnp.bfloat16)
    latent_out = jnp.einsum(
        "sqht,stc->sqhc", weights[..., :CACHE], cache_latent, preferred_element_type=jnp.float32
    )
    latent_out = (
        latent_out
        + jnp.einsum(
            "sqhk,skc->sqhc", weights[..., CACHE:], latent_slots, preferred_element_type=jnp.float32
        )
    ).astype(jnp.bfloat16)
    head_out = jnp.einsum(
        "sqhc,chv->sqhv",
        latent_out,
        value_up.reshape(KVRANK, heads_here, VDIM),
        preferred_element_type=jnp.float32,
    ).astype(jnp.bfloat16)
    request_out = jnp.dot(
        selector, head_out.reshape(seq_count, -1), preferred_element_type=jnp.float32
    )
    request_out = request_out.astype(jnp.bfloat16).reshape(seq_count * NEWTOK, heads_here * VDIM)
    out_rows = lax.all_to_all(out_cast, "tp", split_axis=0, concat_axis=1, tiled=True)
    partial_out = jnp.dot(
        request_out,
        lax.all_gather(out_rows, "dp", axis=1, tiled=True),
        preferred_element_type=jnp.float32,
    )
    reduced = lax.psum_scatter(partial_out, "tp", scatter_dimension=1, tiled=True)
    attention_out = reduced.astype(jnp.bfloat16).reshape(seq_count, NEWTOK, -1)
    return (attention_out, weight_norm)


def solution(mesh):
    in_specs = (
        P("dp", None, None),
        P("dp", None, None),
        P("dp", None, None),
        P("dp", None, None),
        P("dp", None, None),
        P("dp"),
        P("dp", None),
        P(("dp", "tp"), None),
        P(("dp", "tp"), None),
        P(("dp", "tp"), None),
        P(None, ("dp", "tp")),
    )
    out_specs = (P("dp", None, "tp"), P())
    return jax.shard_map(shards, mesh=mesh, in_specs=in_specs, out_specs=out_specs, check_vma=False)
```

profile of v0, /device:TPU:0, one launch (start us, length us, event | category | flops | bytes accessed | tf_op | source)
XLA Modules:
  0.0 955.4 jit_solution(7704429652962988391)
XLA Ops:
  25.6 46.7 %all_to_all.64 = bf16[4,2048,224]{1,2,0:T(8,128)(2,1)} all-to-all(bf16[4,2048,224]{1,2,0:T(8,128)(2,1)S(1)} %bitcast.89), channel_id=1, replica_groups=mesh['dp'=8,'tp'=4] {'tp'}, dimensions={0} | all-to-all | bytes 7340032 | tf_op jit(solution)/shard_map/all_to_all | solution.py:145
  72.3 14.4 %copy.71 = bf16[8,16,8192]{1,0,2:T(8,128)(2,1)} copy(bf16[8,16,8192]{2,1,0:T(8,128)(2,1)} %bitcast.100) | data formatting | bytes 4194304 | tf_op jit(solution)/shard_map/all_gather | solution.py:63
  86.7 20.3 %reshape.140 = bf16[4,2,131072]{2,1,0:T(2,128)(2,1)} reshape(bf16[8192,8,16]{2,1,0:T(8,128)(2,1)} %bitcast.83) | data formatting | bytes 4194304
  111.8 14.4 %copy.82 = bf16[8,16,8192]{1,0,2:T(8,128)(2,1)} copy(bf16[8,16,8192]{2,1,0:T(8,128)(2,1)} %bitcast.101) | data formatting | bytes 4194304 | tf_op jit(solution)/shard_map/all_gather | solution.py:64
  126.2 20.3 %reshape.136 = bf16[4,2,131072]{2,1,0:T(2,128)(2,1)} reshape(bf16[8192,8,16]{2,1,0:T(8,128)(2,1)} %bitcast.84) | data formatting | bytes 4194304
  151.0 99.3 %all-gather.10.cloned.1.call-done = bf16[384,12288]{1,0:T(8,128)(2,1)} async-done(((bf16[48,12288]{1,0:T(8,128)(2,1)}), bf16[384,12288]{1,0:T(8,128)(2,1)}) %all-gather.10.cloned.1.call-update) | async-done | bytes 9437200 | tf_op jit(solution)/shard_map/all_gather | solution.py:62
  250.3 26.1 %copy.67 = bf16[8,48,12288]{1,0,2:T(8,128)(2,1)} copy(bf16[8,48,12288]{2,1,0:T(8,128)(2,1)} %bitcast.92) | data formatting | bytes 18874368 | tf_op jit(solution)/shard_map/all_gather | solution.py:62
  276.4 54.9 %reshape.138 = bf16[4,2,589824]{2,1,0:T(2,128)(2,1)} reshape(bf16[12288,8,48]{2,1,0:T(8,128)(2,1)} %bitcast.81) | data formatting | bytes 18874368
  351.0 13.4 %reshape.141 = bf16[8192,8,16]{2,1,0:T(8,128)(2,1)} reshape(bf16[4,2,131072]{2,1,0:T(2,128)(2,1)S(1)} %all-to-all-done.1) | data formatting | bytes 4194304
  364.4 17.4 %copy.99 = bf16[8,16,4,2048]{3,2,1,0:T(4,128)(2,1)S(1)} copy(bf16[8,16,4,2048]{1,0,3,2:T(8,128)(2,1)} %bitcast.85) | data formatting | bytes 4194304 | tf_op jit(solution)/shard_map/all_to_all | solution.py:68
  385.1 14.3 %reshape.137 = bf16[8192,8,16]{2,1,0:T(8,128)(2,1)} reshape(bf16[4,2,131072]{2,1,0:T(2,128)(2,1)} %all-to-all-done.2) | data formatting | bytes 4194304
  399.4 17.4 %copy.104 = bf16[8,16,4,2048]{3,2,1,0:T(4,128)(2,1)S(1)} copy(bf16[8,16,4,2048]{1,0,3,2:T(8,128)(2,1)} %bitcast.86) | data formatting | bytes 4194304 | tf_op jit(solution)/shard_map/all_to_all | solution.py:69
  420.0 21.6 %all-to-all-done = bf16[4,2,589824]{2,1,0:T(2,128)(2,1)} async-done(((bf16[4,2,589824]{2,1,0:T(2,128)(2,1)}), bf16[4,2,589824]{2,1,0:T(2,128)(2,1)}, u32[]{:S(2)}, u32[]{:S(2)}) %all-to-all-start) | async-done | bytes 9437216 | tf_op jit(solution)/shard_map/all_to_all | solution.py:67
  441.6 40.7 %reshape.139 = bf16[12288,8,48]{2,1,0:T(8,128)(2,1)} reshape(bf16[4,2,589824]{2,1,0:T(2,128)(2,1)} %all-to-all-done) | data formatting | bytes 18874368
  482.3 28.1 %copy.98 = bf16[8,48,4,3072]{3,2,1,0:T(4,128)(2,1)} copy(bf16[8,48,4,3072]{1,0,3,2:T(8,128)(2,1)} %bitcast.82) | data formatting | bytes 18874368 | tf_op jit(solution)/shard_map/all_to_all | solution.py:67
  510.4 10.7 %copy.69 = bf16[8,4,48,3072]{3,2,1,0:T(8,128)(2,1)} copy(bf16[8,4,48,3072]{3,1,2,0:T(4,128)(2,1)} %bitcast.87) | data formatting | bytes 18874368 | tf_op jit(solution)/shard_map/all_to_all | solution.py:67
  553.2 23.9 %fusion.2 = f32[128,4,16,256]{3,2,1,0:T(8,128)} fusion(bf16[128,256,512]{2,1,0:T(8,128)(2,1)} %param.14, bf16[128,4,16,512]{3,0,1,2:T(8,128)(2,1)} %copy-done.3), kind=kOutput, calls=%fused_computation.2 | convolution fusion | flops 2147483648 | bytes 50331648 | tf_op jit(solution)/shard_map/sqhc,stc->sqht/dot_general | solution.py:104
  594.8 21.2 %fusion = f32[128,4,16,512]{3,2,1,0:T(8,128)} fusion(bf16[128,256,512]{2,1,0:T(8,128)(2,1)} %param.14, bf16[128,4,16,260]{3,2,1,0:T(8,128)(2,1)} %divide_convert_fusion), kind=kOutput, calls=%fused_computation | convolution fusion | flops 2147483648 | bytes 54525952 | tf_op jit(solution)/shard_map/sqht,stc->sqhc/dot_general | solution.py:126
  616.0 10.3 %add_convert_fusion = bf16[128,4,16,512]{3,2,1,0:T(8,128)(2,1)} fusion(f32[128,4,16,512]{3,2,1,0:T(8,128)} %fusion, bf16[128,4,16,260]{3,2,1,0:T(8,128)(2,1)} %divide_convert_fusion, bf16[128,4,512,1]{2,1,0,3:T(4,128)(2,1)S(1)} %copy-done.6), kind=kOutput, calls=%fused_computation.4 | convolution fusion | flops 41943040 | bytes 27787264 | tf_op jit(solution)/shard_map/sqhk,skc->sqhc/dot_general | solution.py:131
  626.3 13.6 %convert_bitcast_fusion.1 = bf16[128,4,16,128]{0,3,1,2:T(8,128)(2,1)S(1)} fusion(bf16[512,16,128,1]{2,1,0,3:T(8,128)(2,1)S(1)} %bitcast.102, bf16[128,4,16,512]{3,2,1,0:T(8,128)(2,1)} %add_convert_fusion), kind=kOutput, calls=%fused_computation.34 | convolution fusion | flops 1074790400 | bytes 12582912 | tf_op jit(solution)/shard_map/sqhc,chv->sqhv/dot_general | solution.py:135
  643.7 165.2 %all-gather.8.cloned.1.call-done = bf16[2048,7168]{0,1:T(8,128)(2,1)} async-done(((bf16[2048,896]{0,1:T(8,128)(2,1)}), bf16[2048,7168]{0,1:T(8,128)(2,1)}) %all-gather.8.cloned.1.call-update) | async-done | bytes 29360144 | tf_op jit(solution)/shard_map/all_gather | solution.py:148
  809.0 23.8 %fusion.36 = f32[512,7168]{1,0:T(8,128)} fusion(bf16[512,2048]{1,0:T(8,128)(2,1)} %reshape.123, bf16[2048,7168]{0,1:T(8,128)(2,1)} %all-gather.8.cloned.1.call-done), kind=kOutput, calls=%fused_computation.56 | convolution fusion | flops 15032385536 | bytes 46137344 | tf_op jit(solution)/shard_map/dot_general | solution.py:146
  835.3 39.9 %psum.7 = f32[]{:T(128)} all-reduce(f32[]{:T(128)S(6)} %add.51), channel_id=1, replica_groups=mesh['dp'=8,'tp'=4] {'dp','tp'}, use_global_device_ids=true, to_apply=%region_8.9 | all-reduce | flops 1 | bytes 8 | tf_op jit(solution)/shard_map/psum | solution.py:54
  875.9 67.7 %reduce-scatter.2.cloned.1.call-done = f32[512,1792]{1,0:T(8,128)} async-done(((f32[512,7168]{1,0:T(8,128)}), f32[512,1792]{1,0:T(8,128)}) %reduce-scatter.2.cloned.1.call-update) | async-done | bytes 3670032 | tf_op jit(solution)/shard_map/reduce_scatter | solution.py:151
  (86 shorter events, 110.6 us)
Async XLA Ops:
  7.2 339.5 %copy-start = (bf16[128,4,64]{0,2,1:T(8,128)(2,1)S(1)}, bf16[128,4,64]{0,2,1:T(8,128)(2,1)}, u32[]{:S(2)}) copy-start(bf16[128,4,64]{0,2,1:T(8,128)(2,1)} %param.13) | copy-start | bytes 196612
  7.2 65.1 %all-gather.12.cloned.1.call-start = ((), (), s32[]{:S(2)}) async-start(), calls=%async_computation.8 | async-start | bytes 2359296 | tf_op jit(solution)/shard_map/all_gather | solution.py:63
  9.8 102.0 %all-gather.14.cloned.1.call-start = ((), (), s32[]{:S(2)}) async-start(), calls=%async_computation.9 | async-start | bytes 2359296 | tf_op jit(solution)/shard_map/all_gather | solution.py:64
  12.5 237.9 %all-gather.10.cloned.1.call-start = ((), (), s32[]{:S(2)}) async-start(), calls=%async_computation.7 | async-start | bytes 10616832 | tf_op jit(solution)/shard_map/all_gather | solution.py:62
  17.1 791.9 %all-gather.8.cloned.1.call-start = ((), (), s32[]{:S(2)}) async-start(), calls=%async_computation.5 | async-start | bytes 33030144 | tf_op jit(solution)/shard_map/all_gather | solution.py:148
  107.1 39.5 %all-to-all-start.1 = ((bf16[4,2,131072]{2,1,0:T(2,128)(2,1)}), bf16[4,2,131072]{2,1,0:T(2,128)(2,1)S(1)}, u32[]{:S(2)}, u32[]{:S(2)}) async-start(bf16[4,2,131072]{2,1,0:T(2,128)(2,1)} %reshape.140), calls=%async_computation.1 | async-start | bytes 4194304 | tf_op jit(solution)/shard_map/all_to_all | solution.py:68
  146.6 184.7 %all-to-all-start.2 = ((bf16[4,2,131072]{2,1,0:T(2,128)(2,1)}), bf16[4,2,131072]{2,1,0:T(2,128)(2,1)}, u32[]{:S(2)}, u32[]{:S(2)}) async-start(bf16[4,2,131072]{2,1,0:T(2,128)(2,1)} %reshape.136), calls=%async_computation.2 | async-start | bytes 4194304 | tf_op jit(solution)/shard_map/all_to_all | solution.py:69
  331.3 7.8 copy-start.11
  331.3 110.3 %all-to-all-start = ((bf16[4,2,589824]{2,1,0:T(2,128)(2,1)}), bf16[4,2,589824]{2,1,0:T(2,128)(2,1)}, u32[]{:S(2)}, u32[]{:S(2)}) async-start(bf16[4,2,589824]{2,1,0:T(2,128)(2,1)} %reshape.138), calls=%async_computation | async-start | bytes 18874368 | tf_op jit(solution)/shard_map/all_to_all | solution.py:67
  337.2 606.4 %reduce-scatter.2.cloned.1.call-start = ((), (), s32[]{:S(2)}) async-start(), calls=%async_computation.6 | async-start | bytes 18350080 | tf_op jit(solution)/shard_map/reduce_scatter | solution.py:151
  337.3 7.7 copy-start.10
  339.1 8.8 copy-start.12
  534.8 1.6 slice-start.1
  536.4 0.9 copy-start.8
  537.3 2.0 slice-start
  537.3 2.2 copy-start.5
  539.3 9.9 %copy-start.4 = (bf16[128,4,16,32]{3,2,1,0:T(8,128)(2,1)}, bf16[128,4,16,32]{3,2,1,0:T(8,128)(2,1)S(1)}, u32[]{:S(2)}) copy-start(bf16[128,4,16,32]{3,2,1,0:T(8,128)(2,1)S(1)} %get-tuple-element.5) | copy-start | bytes 1572868
  539.5 4.8 copy-start.6
  544.4 4.8 copy-start.3
  544.4 4.8 copy-start.9
  577.0 8.9 copy-start.2
  616.0 10.4 %copy-start.7 = (bf16[64,8,16,128]{3,2,1,0:T(8,128)(2,1)S(1)}, bf16[64,8,16,128]{3,2,1,0:T(8,128)(2,1)}, u32[]{:S(2)}) copy-start(bf16[64,8,16,128]{3,2,1,0:T(8,128)(2,1)} %copy.112) | copy-start | bytes 6291460
  875.9 71.5 %copy-start.1 = (bf16[128,4,64]{0,2,1:T(8,128)(2,1)S(1)}, bf16[128,4,64]{0,2,1:T(8,128)(2,1)}, u32[]{:S(2)}) copy-start(bf16[128,4,64]{0,2,1:T(8,128)(2,1)} %param.13) | copy-start | bytes 196612
Sparse Core Ops, SparseCore 0:
  10.1 51.7 all-gather.11
  64.1 47.6 all-gather.13
  114.5 135.7 all-gather.9
  251.7 557.1 all-gather.7
  832.9 110.7 reduce-scatter.1
where the time goes:
time: 965 us; the launch traced here: 955 us
  waiting for transfers between devices  355 us (37%)
  local copies, waits for them, and re-layouts  320 us (33%)
  matrix products  126 us (13%)
  blocking collectives  86.6 us (9%)
  other arithmetic  34.3 us (4%)
  between operations  18.9 us (2%)
  starting transfers between devices  14.4 us (1%)
    unnamed x36, local copies, waits for them, and re-layouts  171 us
    all_gather x1, waiting for transfers between devices, shards(): lax.all_gather(out_rows, 'dp', axis=1, tiled=True)  165 us
    all_gather x1, waiting for transfers between devices, shards(): lax.all_gather(query_cast[None], 'dp', axis=0, tiled=True)  99.3 us
    reduce_scatter x1, waiting for transfers between devices, shards(): lax.psum_scatter(partial_out, 'tp', scatter_dimension=1, tiled=True)  67.7 us
    all_to_all x1, blocking collectives, shards(): lax.all_to_all(out_cast, 'tp', split_axis=0, concat_axis=1, tiled=True)  46.7 us
    psum x1, blocking collectives, shards(): squares_total = lax.psum(local_squares, ('dp', 'tp'))  39.9 us
    all_to_all x2, local copies, waits for them, and re-layouts, shards(): lax.all_to_all(gathered[0], 'tp', split_axis=2, concat_axis=1, tiled=True)  38.7 us
    all_gather x1, local copies, waits for them, and re-layouts, shards(): lax.all_gather(query_cast[None], 'dp', axis=0, tiled=True)  26.1 us
  transfers between devices with their start and end apart: 8, of which 5 were waited for; matrix products, arithmetic and copies ran while one was open for 47% of the time, Pallas kernels for 0%

commit v1 on v0

--- a/solution.py
+++ b/solution.py
@@ -59,7 +59,9 @@
     key_cast = w_uk.astype(jnp.bfloat16)
     value_cast = w_uv.astype(jnp.bfloat16)
     gathered = (
-        lax.all_gather(query_cast[None], "dp", axis=0, tiled=True),
+        jnp.concatenate(
+            lax.all_to_all(jnp.stack([query_cast[None]] * lax.axis_size("dp")), "dp", 0, 0), axis=0
+        ),
         lax.all_gather(key_cast[None], "dp", axis=0, tiled=True),
         lax.all_gather(value_cast[None], "dp", axis=0, tiled=True),
     )

time: 965 us -> 1050 us (1.088)
  blocking collectives: 86.6 us -> 154 us
  waiting for transfers between devices: 355 us -> 366 us
    all_to_all x0 -> x1, waiting for transfers between devices: none -> 255 us  [shards(): lax.all_to_all(jnp.stack([query_cast[None]] * lax.axis_size('dp')), 'dp',...]
    all_gather x1, waiting for transfers between devices: 165 us -> 0.01 us  [shards(): lax.all_gather(out_rows, 'dp', axis=1, tiled=True)]
    all_gather x1 -> x0, waiting for transfers between devices: 99.3 us -> none  [shards(): lax.all_gather(query_cast[None], 'dp', axis=0, tiled=True)]
    psum x1, blocking collectives: 39.9 us -> 107 us  [shards(): squares_total = lax.psum(local_squares, ('dp', 'tp'))]
    all_gather x1 -> x0, local copies, waits for them, and re-layouts: 26.1 us -> none  [shards(): lax.all_gather(query_cast[None], 'dp', axis=0, tiled=True)]
    reshape x0 -> x1, local copies, waits for them, and re-layouts: none -> 26.1 us  [shards(): jnp.concatenate(lax.all_to_all(jnp.stack([query_cast[None]] * lax.axis_si...]
    all_to_all x1, waiting for transfers between devices: 0.01 us -> 22 us  [shards(): lax.all_to_all(gathered[1], 'tp', split_axis=2, concat_axis=1, tiled=True)]
  transfers between devices with their start and end apart: 8 -> 8, of which waited for: 5 -> 4; matrix products, arithmetic and copies ran while one was open for 47% -> 43% of each run, Pallas kernels for 0% -> 0%
where the time goes in v1:
time: 1050 us; the launch traced here: 1040 us
  waiting for transfers between devices  366 us (35%)
  local copies, waits for them, and re-layouts  325 us (31%)
  blocking collectives  154 us (15%)
  matrix products  126 us (12%)
  other arithmetic  33.2 us (3%)
  starting transfers between devices  20.9 us (2%)
  between operations  18.8 us (2%)
    all_to_all x1, waiting for transfers between devices, shards(): lax.all_to_all(jnp.stack([query_cast[None]] * lax.axis_size('dp')), 'dp',...  255 us
    unnamed x36, local copies, waits for them, and re-layouts  171 us
    psum x1, blocking collectives, shards(): squares_total = lax.psum(local_squares, ('dp', 'tp'))  107 us
    reduce_scatter x1, waiting for transfers between devices, shards(): lax.psum_scatter(partial_out, 'tp', scatter_dimension=1, tiled=True)  67.6 us
    all_to_all x1, blocking collectives, shards(): lax.all_to_all(out_cast, 'tp', split_axis=0, concat_axis=1, tiled=True)  46.7 us
    all_to_all x2, local copies, waits for them, and re-layouts, shards(): lax.all_to_all(gathered[0], 'tp', split_axis=2, concat_axis=1, tiled=True)  38.7 us
    reshape x1, local copies, waits for them, and re-layouts, shards(): jnp.concatenate(lax.all_to_all(jnp.stack([query_cast[None]] * lax.axis_si...  26.1 us
    dot_general x1, matrix products, shards(): jnp.dot(request_out, lax.all_gather(out_rows, 'dp', axis=1, tiled=True),...  23.8 us
  transfers between devices with their start and end apart: 8, of which 4 were waited for; matrix products, arithmetic and copies ran while one was open for 43% of the time, Pallas kernels for 0%

profile of v1, /device:TPU:0, one launch (start us, length us, event | category | flops | bytes accessed | tf_op | source)
XLA Modules:
  0.0 1043.4 jit_solution(10515301430527426883)
XLA Ops:
  20.6 46.7 %all_to_all.69 = bf16[4,2048,224]{1,2,0:T(8,128)(2,1)} all-to-all(bf16[4,2048,224]{1,2,0:T(8,128)(2,1)S(1)} %bitcast.89), channel_id=1, replica_groups=mesh['dp'=8,'tp'=4] {'tp'}, dimensions={0} | all-to-all | bytes 7340032 | tf_op jit(solution)/shard_map/all_to_all | solution.py:147
  67.4 14.5 %copy.71 = bf16[8,16,8192]{1,0,2:T(8,128)(2,1)} copy(bf16[8,16,8192]{2,1,0:T(8,128)(2,1)} %bitcast.100) | data formatting | bytes 4194304 | tf_op jit(solution)/shard_map/all_gather | solution.py:65
  81.8 20.4 %reshape.145 = bf16[4,2,131072]{2,1,0:T(2,128)(2,1)} reshape(bf16[8192,8,16]{2,1,0:T(8,128)(2,1)} %bitcast.83) | data formatting | bytes 4194304
  109.4 22.0 %all-to-all-done.2 = bf16[4,2,131072]{2,1,0:T(2,128)(2,1)S(1)} async-done(((bf16[4,2,131072]{2,1,0:T(2,128)(2,1)}), bf16[4,2,131072]{2,1,0:T(2,128)(2,1)S(1)}, u32[]{:S(2)}, u32[]{:S(2)}) %all-to-all-start.2) | async-done | bytes 2097184 | tf_op jit(solution)/shard_map/all_to_all | solution.py:70
  143.0 14.4 %copy.82 = bf16[8,16,8192]{1,0,2:T(8,128)(2,1)} copy(bf16[8,16,8192]{2,1,0:T(8,128)(2,1)} %bitcast.99) | data formatting | bytes 4194304 | tf_op jit(solution)/shard_map/all_gather | solution.py:66
  157.4 20.3 %reshape.141 = bf16[4,2,131072]{2,1,0:T(2,128)(2,1)} reshape(bf16[8192,8,16]{2,1,0:T(8,128)(2,1)} %bitcast.84) | data formatting | bytes 4194304
  177.8 255.0 %all-to-all-done = bf16[8,1,48,12288]{3,2,1,0:T(8,128)(2,1)} async-done(((bf16[8,1,48,12288]{3,2,1,0:T(8,128)(2,1)}), bf16[8,1,48,12288]{3,2,1,0:T(8,128)(2,1)}, u32[]{:S(2)}, u32[]{:S(2)}) %all-to-all-start) | async-done | bytes 9437216 | tf_op jit(solution)/shard_map/all_to_all | solution.py:63
  437.2 26.1 %copy.67 = bf16[8,48,12288]{1,0,2:T(8,128)(2,1)} copy(bf16[8,48,12288]{2,1,0:T(8,128)(2,1)} %bitcast.1) | data formatting | bytes 18874368 | tf_op jit(solution)/shard_map/reshape | solution.py:62
  463.3 54.9 %reshape.143 = bf16[4,2,589824]{2,1,0:T(2,128)(2,1)} reshape(bf16[12288,8,48]{2,1,0:T(8,128)(2,1)} %bitcast.81) | data formatting | bytes 18874368
  538.0 13.5 %reshape.146 = bf16[8192,8,16]{2,1,0:T(8,128)(2,1)} reshape(bf16[4,2,131072]{2,1,0:T(2,128)(2,1)S(1)} %all-to-all-done.2) | data formatting | bytes 4194304
  551.4 17.4 %copy.99 = bf16[8,16,4,2048]{3,2,1,0:T(4,128)(2,1)S(1)} copy(bf16[8,16,4,2048]{1,0,3,2:T(8,128)(2,1)} %bitcast.85) | data formatting | bytes 4194304 | tf_op jit(solution)/shard_map/all_to_all | solution.py:70
  572.1 14.4 %reshape.142 = bf16[8192,8,16]{2,1,0:T(8,128)(2,1)} reshape(bf16[4,2,131072]{2,1,0:T(2,128)(2,1)} %all-to-all-done.3) | data formatting | bytes 4194304
  586.4 17.4 %copy.104 = bf16[8,16,4,2048]{3,2,1,0:T(4,128)(2,1)S(1)} copy(bf16[8,16,4,2048]{1,0,3,2:T(8,128)(2,1)} %bitcast.86) | data formatting | bytes 4194304 | tf_op jit(solution)/shard_map/all_to_all | solution.py:71
  607.0 21.6 %all-to-all-done.1 = bf16[4,2,589824]{2,1,0:T(2,128)(2,1)} async-done(((bf16[4,2,589824]{2,1,0:T(2,128)(2,1)}), bf16[4,2,589824]{2,1,0:T(2,128)(2,1)}, u32[]{:S(2)}, u32[]{:S(2)}) %all-to-all-start.1) | async-done | bytes 9437216 | tf_op jit(solution)/shard_map/all_to_all | solution.py:69
  628.6 40.7 %reshape.144 = bf16[12288,8,48]{2,1,0:T(8,128)(2,1)} reshape(bf16[4,2,589824]{2,1,0:T(2,128)(2,1)} %all-to-all-done.1) | data formatting | bytes 18874368
  669.3 28.0 %copy.98 = bf16[8,48,4,3072]{3,2,1,0:T(4,128)(2,1)} copy(bf16[8,48,4,3072]{1,0,3,2:T(8,128)(2,1)} %bitcast.82) | data formatting | bytes 18874368 | tf_op jit(solution)/shard_map/all_to_all | solution.py:69
  697.3 10.7 %copy.69 = bf16[8,4,48,3072]{3,2,1,0:T(8,128)(2,1)} copy(bf16[8,4,48,3072]{3,1,2,0:T(4,128)(2,1)} %bitcast.87) | data formatting | bytes 18874368 | tf_op jit(solution)/shard_map/all_to_all | solution.py:69
  740.1 23.1 %fusion.2 = f32[128,4,16,256]{3,2,1,0:T(8,128)} fusion(bf16[128,256,512]{2,1,0:T(8,128)(2,1)} %param.14, bf16[128,4,16,512]{3,0,1,2:T(8,128)(2,1)} %copy-done.3), kind=kOutput, calls=%fused_computation.2 | convolution fusion | flops 2147483648 | bytes 50331648 | tf_op jit(solution)/shard_map/sqhc,stc->sqht/dot_general | solution.py:106
  781.0 21.0 %fusion = f32[128,4,16,512]{3,2,1,0:T(8,128)} fusion(bf16[128,256,512]{2,1,0:T(8,128)(2,1)} %param.14, bf16[128,4,16,260]{3,2,1,0:T(8,128)(2,1)} %divide_convert_fusion), kind=kOutput, calls=%fused_computation | convolution fusion | flops 2147483648 | bytes 54525952 | tf_op jit(solution)/shard_map/sqht,stc->sqhc/dot_general | solution.py:128
  802.1 10.4 add_convert_fusion
  812.4 13.6 %convert_bitcast_fusion.1 = bf16[128,4,16,128]{0,3,1,2:T(8,128)(2,1)S(1)} fusion(bf16[512,16,128,1]{2,1,0,3:T(8,128)(2,1)S(1)} %bitcast.101, bf16[128,4,16,512]{3,2,1,0:T(8,128)(2,1)} %add_convert_fusion), kind=kOutput, calls=%fused_computation.34 | convolution fusion | flops 1074790400 | bytes 12582912 | tf_op jit(solution)/shard_map/sqhc,chv->sqhv/dot_general | solution.py:137
  829.8 23.8 %fusion.36 = f32[512,7168]{1,0:T(8,128)} fusion(bf16[512,2048]{1,0:T(8,128)(2,1)} %reshape.129, bf16[2048,7168]{0,1:T(8,128)(2,1)} %all-gather.6.cloned.1.call-done), kind=kOutput, calls=%fused_computation.56 | convolution fusion | flops 15032385536 | bytes 46137344 | tf_op jit(solution)/shard_map/dot_general | solution.py:148
  856.0 107.3 %psum.7 = f32[]{:T(128)} all-reduce(f32[]{:T(128)S(6)} %add.51), channel_id=1, replica_groups=mesh['dp'=8,'tp'=4] {'dp','tp'}, use_global_device_ids=true, to_apply=%region_8.9 | all-reduce | flops 1 | bytes 8 | tf_op jit(solution)/shard_map/psum | solution.py:54
  964.0 67.6 %reduce-scatter.2.cloned.1.call-done = f32[512,1792]{1,0:T(8,128)} async-done(((f32[512,7168]{1,0:T(8,128)}), f32[512,1792]{1,0:T(8,128)}) %reduce-scatter.2.cloned.1.call-update) | async-done | bytes 3670032 | tf_op jit(solution)/shard_map/reduce_scatter | solution.py:153
  (86 shorter events, 119.9 us)
Async XLA Ops:
  7.2 526.5 %copy-start = (bf16[128,4,64]{0,2,1:T(8,128)(2,1)S(1)}, bf16[128,4,64]{0,2,1:T(8,128)(2,1)}, u32[]{:S(2)}) copy-start(bf16[128,4,64]{0,2,1:T(8,128)(2,1)} %param.13) | copy-start | bytes 196612
  7.2 60.2 %all-gather.8.cloned.1.call-start = ((), (), s32[]{:S(2)}) async-start(), calls=%async_computation.8 | async-start | bytes 2359296 | tf_op jit(solution)/shard_map/all_gather | solution.py:65
  9.8 133.2 %all-gather.10.cloned.1.call-start = ((), (), s32[]{:S(2)}) async-start(), calls=%async_computation.9 | async-start | bytes 2359296 | tf_op jit(solution)/shard_map/all_gather | solution.py:66
  12.5 817.3 %all-gather.6.cloned.1.call-start = ((), (), s32[]{:S(2)}) async-start(), calls=%async_computation.6 | async-start | bytes 33030144 | tf_op jit(solution)/shard_map/all_gather | solution.py:150
  102.2 29.3 %all-to-all-start.2 = ((bf16[4,2,131072]{2,1,0:T(2,128)(2,1)}), bf16[4,2,131072]{2,1,0:T(2,128)(2,1)S(1)}, u32[]{:S(2)}, u32[]{:S(2)}) async-start(bf16[4,2,131072]{2,1,0:T(2,128)(2,1)} %reshape.145), calls=%async_computation.2 | async-start | bytes 4194304 | tf_op jit(solution)/shard_map/all_to_all | solution.py:70
  136.2 296.6 %all-to-all-start = ((bf16[8,1,48,12288]{3,2,1,0:T(8,128)(2,1)}), bf16[8,1,48,12288]{3,2,1,0:T(8,128)(2,1)}, u32[]{:S(2)}, u32[]{:S(2)}) async-start(bf16[8,1,48,12288]{3,2,1,0:T(8,128)(2,1)} %stack.3), calls=%async_computation | async-start | bytes 18874368 | tf_op jit(solution)/shard_map/all_to_all | solution.py:63
  432.8 85.5 %all-to-all-start.3 = ((bf16[4,2,131072]{2,1,0:T(2,128)(2,1)}), bf16[4,2,131072]{2,1,0:T(2,128)(2,1)}, u32[]{:S(2)}, u32[]{:S(2)}) async-start(bf16[4,2,131072]{2,1,0:T(2,128)(2,1)} %reshape.141), calls=%async_computation.3 | async-start | bytes 4194304 | tf_op jit(solution)/shard_map/all_to_all | solution.py:71
  518.3 7.8 copy-start.11
  518.3 110.3 %all-to-all-start.1 = ((bf16[4,2,589824]{2,1,0:T(2,128)(2,1)}), bf16[4,2,589824]{2,1,0:T(2,128)(2,1)}, u32[]{:S(2)}, u32[]{:S(2)}) async-start(bf16[4,2,589824]{2,1,0:T(2,128)(2,1)} %reshape.143), calls=%async_computation.1 | async-start | bytes 18874368 | tf_op jit(solution)/shard_map/all_to_all | solution.py:69
  524.2 507.5 %reduce-scatter.2.cloned.1.call-start = ((), (), s32[]{:S(2)}) async-start(), calls=%async_computation.7 | async-start | bytes 18350080 | tf_op jit(solution)/shard_map/reduce_scatter | solution.py:153
  524.2 7.7 copy-start.10
  526.0 8.8 copy-start.12
  721.7 1.6 slice-start.1
  723.3 0.9 copy-start.8
  724.2 2.0 slice-start
  724.2 2.2 copy-start.5
  726.2 9.9 copy-start.4
  726.5 4.8 copy-start.6
  731.3 4.8 copy-start.3
  731.3 4.8 copy-start.9
  763.2 8.9 copy-start.2
  802.1 10.4 copy-start.7
  964.0 71.3 %copy-start.1 = (bf16[128,4,64]{0,2,1:T(8,128)(2,1)S(1)}, bf16[128,4,64]{0,2,1:T(8,128)(2,1)}, u32[]{:S(2)}) copy-start(bf16[128,4,64]{0,2,1:T(8,128)(2,1)} %param.13) | copy-start | bytes 196612
Sparse Core Ops, SparseCore 0:
  10.1 51.8 all-gather.7
  64.7 47.6 all-gather.9
  114.0 665.0 all-gather.5
  853.7 177.9 reduce-scatter.1
